TPU v7x, 512 devices: a whole 4x8x8 slice. The times are simulated.
512 devices in a mesh: unit: 2 (over y_1), row: 16 (over y_0, x, core), col: 16 (over z, y_2).
Axes of the slice: x: 4, y: 8 (y_0: 2, y_1: 2, y_2: 2; y = y_0 * 4 + y_1 * 2 + y_2), z: 8, core: 2. Of those that a mesh axis runs over, the one named last changes fastest.
Arguments:
- tracer: float32 [4, 128, 256, 256], P('unit', None, 'row', 'col'), parts along dimension 0, may hold values from -6 to 6
- symbol_x: float32 [128], replicated, may hold values from 0.3 to 3
- symbol_y: float32 [256], replicated, may hold values from 0.3 to 3
- symbol_z: float32 [256], replicated, may hold values from 0.3 to 3
Outputs:
- smoothed: float32 [4, 128, 256, 256], P('unit', None, 'row', 'col'), parts along dimension 0
There are 2 independent parts, one for each index of `unit`. A program takes and returns all parts, laid end to end along the dimension named above; an argument that names none is the same for every part. Nothing has to cross between parts.
All inputs are finite; a program needn't handle non-finite values.
Results may differ from a plain program's by a relative error of at most 0.0003.
Values sent between devices are 32-bit elements.
A program may use at most 64 MiB of HBM per device.

v0:
```python
import jax
import jax.numpy as jnp
from jax import lax
from jax.sharding import PartitionSpec as P


def mode_table(count):
    rank = jnp.arange(count)
    angle = (
        jnp.pi
        / (4 * count)
        * ((2 * rank[:, None] + 1) * (2 * rank[None, :] + 1) % (8 * count)).astype(jnp.float32)
    )
    return jnp.cos(angle) * (2.0 / count) ** 0.5


def to_modes(values, dim):
    moved = jnp.tensordot(
        values, mode_table(values.shape[dim]), axes=([dim], [0]), precision=lax.Precision.HIGHEST
    )
    return jnp.moveaxis(moved, -1, dim)


def shards(tracer, symbol_x, symbol_y, symbol_z):

    def forward_part(part_values):
        part_values = to_modes(part_values, 1)
        part_values = lax.all_to_all(part_values, "row", split_axis=1, concat_axis=2, tiled=True)
        part_values = to_modes(part_values, 2)
        part_values = lax.all_to_all(part_values, "col", split_axis=2, concat_axis=3, tiled=True)
        return to_modes(part_values, 3)

    def backward_part(part_values):
        part_values = to_modes(part_values, 3)
        part_values = lax.all_to_all(part_values, "col", split_axis=3, concat_axis=2, tiled=True)
        part_values = to_modes(part_values, 2)
        part_values = lax.all_to_all(part_values, "row", split_axis=2, concat_axis=1, tiled=True)
        return to_modes(part_values, 1)

    block_values = forward_part(tracer)
    share_x = block_values.shape[1]
    part_x = lax.dynamic_slice_in_dim(symbol_x, lax.axis_index("row") * share_x, share_x)
    share_y = block_values.shape[2]
    part_y = lax.dynamic_slice_in_dim(symbol_y, lax.axis_index("col") * share_y, share_y)
    symbol = part_x[:, None, None] + part_y[None, :, None] + symbol_z[None, None, :]
    block_values = block_values * lax.rsqrt(symbol)
    block_values = backward_part(block_values)
    return block_values


def solution(mesh):
    in_specs = (P("unit", None, "row", "col"), P(), P(), P())
    out_specs = P("unit", None, "row", "col")
    return jax.shard_map(shards, mesh=mesh, in_specs=in_specs, out_specs=out_specs, check_vma=False)
```

profile of v0, /device:TPU:8, one launch (start us, length us, event | category | flops | bytes accessed | tf_op | source)
XLA Modules:
  0.0 125.6 jit_solution(17801068232473638482)
XLA Ops:
  0.0 0.0 copy-start
  0.0 0.9 copy-done
  1.0 0.7 fusion.51
  1.6 1.8 %copy.14 = f32[2,128,16,16]{3,2,0,1:T(8,128)S(1)} copy(f32[2,128,16,16]{1,3,2,0:T(8,128)S(1)} %bitcast.75) | data formatting | bytes 524288 | tf_op jit(solution)/shard_map/transpose | solution.py:21
  3.5 1.5 %reshape.67 = f32[16,1,4096]{2,1,0:T(1,128)} reshape(f32[128,2,16,16]{3,2,1,0:T(8,128)S(1)} %bitcast.64) | data formatting | bytes 524288
  4.9 8.8 %all-to-all-start = ((f32[16,1,4096]{2,1,0:T(1,128)}), f32[16,1,4096]{2,1,0:T(1,128)S(1)}, u32[]{:S(2)}, u32[]{:S(2)}) async-start(f32[16,1,4096]{2,1,0:T(1,128)} %reshape.67), calls=%async_computation | async-start | bytes 524288 | tf_op jit(solution)/shard_map/all_to_all | solution.py:28
  13.7 15.1 %all-to-all-done = f32[16,1,4096]{2,1,0:T(1,128)S(1)} async-done(((f32[16,1,4096]{2,1,0:T(1,128)}), f32[16,1,4096]{2,1,0:T(1,128)S(1)}, u32[]{:S(2)}, u32[]{:S(2)}) %all-to-all-start) | async-done | bytes 262176 | tf_op jit(solution)/shard_map/all_to_all | solution.py:28
  28.9 0.5 broadcast.193
  29.4 1.2 reduce
  30.6 0.7 reshape.68
  31.3 2.0 %copy.16 = f32[2,8,16,16,16]{3,2,4,1,0:T(8,128)} copy(f32[2,8,16,16,16]{4,3,0,1,2:T(8,128)S(1)} %bitcast.69) | data formatting | bytes 524288 | tf_op jit(solution)/shard_map/all_to_all | solution.py:28
  33.4 2.4 %all_to_all.55 = f32[2,8,256,16]{2,3,1,0:T(8,128)S(1)} reshape(f32[2,8,16,16,16]{3,2,4,1,0:T(8,128)} %copy.16) | data formatting | bytes 524288 | tf_op jit(solution)/shard_map/all_to_all | solution.py:28
  35.8 1.4 %convolution_bitcast_fusion.1 = f32[2,8,256,16]{2,3,1,0:T(8,128)S(1)} fusion(f32[2,8,256,16]{2,3,1,0:T(8,128)S(1)} %all_to_all.55, s32[256]{0:T(256)S(1)} %multiply_add_fusion), kind=kOutput, calls=%fused_computation.6 | convolution fusion | flops 202309632 | bytes 525312 | tf_op jit(solution)/shard_map/dot_general | solution.py:18
  37.3 0.0 copy-start.2
  37.3 0.0 copy-start.3
  37.3 0.0 copy-start.1
  37.3 1.3 %copy.17 = f32[2,8,256,16]{3,1,0,2:T(8,128)S(1)} copy(f32[2,8,256,16]{2,3,1,0:T(8,128)S(1)} %convolution_bitcast_fusion.1) | data formatting | bytes 524288 | tf_op jit(solution)/shard_map/transpose | solution.py:21
  38.6 1.5 %reshape.69 = f32[16,1,4096]{2,1,0:T(1,128)} reshape(f32[256,2,8,16]{3,2,1,0:T(8,128)S(1)} %bitcast.65) | data formatting | bytes 524288
  40.0 11.8 %all-to-all-start.1 = ((f32[16,1,4096]{2,1,0:T(1,128)}), f32[16,1,4096]{2,1,0:T(1,128)S(1)}, u32[]{:S(2)}, u32[]{:S(2)}) async-start(f32[16,1,4096]{2,1,0:T(1,128)} %reshape.69), calls=%async_computation.1 | async-start | bytes 524288 | tf_op jit(solution)/shard_map/all_to_all | solution.py:30
  51.8 0.0 copy-done.2
  51.8 0.1 dynamic_slice.7
  51.9 0.0 copy-done.3
  51.9 0.1 dynamic_slice.6
  52.0 0.1 broadcast_add_fusion
  52.1 0.0 copy-done.1
  52.1 0.1 add_rsqrt_fusion
  52.2 10.2 %all-to-all-done.1 = f32[16,1,4096]{2,1,0:T(1,128)S(1)} async-done(((f32[16,1,4096]{2,1,0:T(1,128)}), f32[16,1,4096]{2,1,0:T(1,128)S(1)}, u32[]{:S(2)}, u32[]{:S(2)}) %all-to-all-start.1) | async-done | bytes 262176 | tf_op jit(solution)/shard_map/all_to_all | solution.py:30
  62.4 1.2 reduce.1
  63.6 0.7 reshape.70
  64.3 2.6 %copy.34 = f32[2,8,16,16,16]{4,2,3,1,0:T(8,128)} copy(f32[2,8,16,16,16]{4,1,0,3,2:T(8,128)S(1)} %bitcast.70) | data formatting | bytes 524288 | tf_op jit(solution)/shard_map/all_to_all | solution.py:30
  66.9 2.4 %all_to_all.59 = f32[2,8,16,256]{3,2,1,0:T(8,128)S(1)} reshape(f32[2,8,16,16,16]{4,3,2,1,0:T(8,128)} %bitcast.71) | data formatting | bytes 524288 | tf_op jit(solution)/shard_map/all_to_all | solution.py:30
  69.3 1.4 %convolution_multiply_fusion = f32[2,8,16,256]{3,2,1,0:T(8,128)S(1)} fusion(f32[2,8,16,256]{3,2,1,0:T(8,128)S(1)} %all_to_all.59, f32[8,16,256]{2,1,0:T(8,128)S(1)} %add_rsqrt_fusion, s32[256]{0:T(256)S(1)} %multiply_add_fusion), kind=kOutput, calls=%fused_computation.5 | convolution fusion | flops 202375168 | bytes 656384 | tf_op jit(solution)/shard_map/dot_general | solution.py:18
  70.8 1.4 %fusion.12 = f32[2,8,16,256]{3,2,1,0:T(8,128)S(1)} fusion(f32[2,8,16,256]{3,2,1,0:T(8,128)S(1)} %convolution_multiply_fusion, s32[256]{0:T(256)S(1)} %multiply_add_fusion), kind=kOutput, calls=%fused_computation.19 | convolution fusion | flops 202309632 | bytes 525312 | tf_op jit(solution)/shard_map/dot_general | solution.py:18
  72.2 1.3 %copy.19 = f32[2,8,16,256]{2,1,0,3:T(8,128)S(1)} copy(f32[2,8,16,256]{3,2,1,0:T(8,128)S(1)} %fusion.12) | data formatting | bytes 524288 | tf_op jit(solution)/shard_map/dot_general | solution.py:18
  73.5 0.7 reshape.71
  74.2 14.5 %all_to_all.72 = f32[16,1,4096]{2,1,0:T(1,128)S(1)} all-to-all(f32[16,1,4096]{2,1,0:T(1,128)S(1)} %reshape.71), channel_id=1, replica_groups=mesh['unit'=2,'row'=16,'col'=16] {'col'}, dimensions={0} | all-to-all | bytes 524288 | tf_op jit(solution)/shard_map/all_to_all | solution.py:35
  88.7 1.2 reduce.2
  89.9 0.7 reshape.72
  90.6 2.6 %copy.33 = f32[2,8,16,16,16]{2,3,4,1,0:T(8,128)} copy(f32[2,8,16,16,16]{2,1,0,4,3:T(8,128)S(1)} %bitcast.72) | data formatting | bytes 524288 | tf_op jit(solution)/shard_map/all_to_all | solution.py:35
  93.2 2.4 %all_to_all.63 = f32[2,8,256,16]{2,3,1,0:T(8,128)S(1)} reshape(f32[2,8,16,16,16]{3,2,4,1,0:T(8,128)} %bitcast.73) | data formatting | bytes 524288 | tf_op jit(solution)/shard_map/all_to_all | solution.py:35
  95.7 1.4 %convolution_bitcast_fusion = f32[2,8,256,16]{2,3,1,0:T(8,128)S(1)} fusion(f32[2,8,256,16]{2,3,1,0:T(8,128)S(1)} %all_to_all.63, s32[256]{0:T(256)S(1)} %multiply_add_fusion), kind=kOutput, calls=%fused_computation.4 | convolution fusion | flops 202309632 | bytes 525312 | tf_op jit(solution)/shard_map/dot_general | solution.py:18
  97.1 1.3 %copy.21 = f32[2,8,256,16]{3,1,0,2:T(8,128)S(1)} copy(f32[2,8,256,16]{2,3,1,0:T(8,128)S(1)} %convolution_bitcast_fusion) | data formatting | bytes 524288 | tf_op jit(solution)/shard_map/transpose | solution.py:21
  98.4 0.7 reshape.73
  99.1 19.3 %all_to_all.73 = f32[16,1,4096]{2,1,0:T(1,128)S(1)} all-to-all(f32[16,1,4096]{2,1,0:T(1,128)S(1)} %reshape.73), channel_id=1, replica_groups=mesh['unit'=2,'row'=16,'col'=16] {'row'}, dimensions={0} | all-to-all | bytes 524288 | tf_op jit(solution)/shard_map/all_to_all | solution.py:37
  118.4 1.2 reduce.3
  119.7 0.7 reshape.74
  120.4 0.7 copy.22
  121.1 4.5 %fusion.2 = f32[2,128,16,16]{1,3,2,0:T(8,128)} fusion(f32[2,128,16,16]{3,2,1,0:T(8,128)S(1)} %bitcast.68, s32[128]{0:T(128)S(1)} %multiply_add_fusion.1), kind=kOutput, calls=%fused_computation.7 | convolution fusion | flops 100909056 | bytes 524800 | tf_op jit(solution)/shard_map/dot_general | solution.py:18
  (2 shorter events, 0.0 us)
Async XLA Ops:
  0.0 1.0 copy-start
  4.9 23.9 %all-to-all-start = ((f32[16,1,4096]{2,1,0:T(1,128)}), f32[16,1,4096]{2,1,0:T(1,128)S(1)}, u32[]{:S(2)}, u32[]{:S(2)}) async-start(f32[16,1,4096]{2,1,0:T(1,128)} %reshape.67), calls=%async_computation | async-start | bytes 524288 | tf_op jit(solution)/shard_map/all_to_all | solution.py:28
  37.3 14.6 %copy-start.2 = (f32[256]{0:T(256)S(1)}, f32[256]{0:T(256)}, u32[]{:S(2)}) copy-start(f32[256]{0:T(256)} %param.6) | copy-start | bytes 3076
  37.3 14.7 %copy-start.3 = (f32[128]{0:T(128)S(1)}, f32[128]{0:T(128)}, u32[]{:S(2)}) copy-start(f32[128]{0:T(128)} %param.5) | copy-start | bytes 1540
  37.3 14.8 %copy-start.1 = (f32[256]{0:T(256)S(1)}, f32[256]{0:T(256)}, u32[]{:S(2)}) copy-start(f32[256]{0:T(256)} %param.7) | copy-start | bytes 3076
  40.0 22.3 %all-to-all-start.1 = ((f32[16,1,4096]{2,1,0:T(1,128)}), f32[16,1,4096]{2,1,0:T(1,128)S(1)}, u32[]{:S(2)}, u32[]{:S(2)}) async-start(f32[16,1,4096]{2,1,0:T(1,128)} %reshape.69), calls=%async_computation.1 | async-start | bytes 524288 | tf_op jit(solution)/shard_map/all_to_all | solution.py:30
where the time goes:
time: 126 us
  blocking collectives  33.8 us (27%)
  local copies, waits for them, and re-layouts  29.7 us (24%)
  waiting for transfers between devices  25.4 us (20%)
  starting transfers between devices  20.6 us (16%)
  matrix products  10.8 us (9%)
  other arithmetic  5.09 us (4%)
    all_to_all x1, blocking collectives, backward_part(): lax.all_to_all(part_values, 'row', split_axis=2, concat_axis=1, tiled=True)  19.3 us
    all_to_all x1, waiting for transfers between devices, forward_part(): lax.all_to_all(part_values, 'row', split_axis=1, concat_axis=2, tiled=True)  15.1 us
    all_to_all x1, blocking collectives, backward_part(): lax.all_to_all(part_values, 'col', split_axis=3, concat_axis=2, tiled=True)  14.5 us
    all_to_all x1, starting transfers between devices, forward_part(): lax.all_to_all(part_values, 'col', split_axis=2, concat_axis=3, tiled=True)  11.8 us
    all_to_all x1, waiting for transfers between devices, forward_part(): lax.all_to_all(part_values, 'col', split_axis=2, concat_axis=3, tiled=True)  10.2 us
    dot_general x5, matrix products, to_modes(): jnp.tensordot(values, mode_table(values.shape[dim]), axes=([dim], [0]), p...  10.1 us
    all_to_all x1, starting transfers between devices, forward_part(): lax.all_to_all(part_values, 'row', split_axis=1, concat_axis=2, tiled=True)  8.77 us
    unnamed x16, local copies, waits for them, and re-layouts  8.21 us
  transfers between devices with their start and end apart: 2, of which 2 were waited for; matrix products, arithmetic and copies ran while one was open for 0% of the time, Pallas kernels for 0%

commit v1 on v0

v1 whole, which is shorter than its diff:
```python
import functools

import jax
import jax.numpy as jnp
import ml_dtypes
import numpy as np
from jax import lax
from jax.experimental import pallas as pl
from jax.experimental.pallas import tpu as pltpu
from jax.sharding import PartitionSpec as P

MESH = pl.DeviceIdType.MESH
F32 = jnp.float32
BF16 = jnp.bfloat16


def cosines(count):
    rank = np.arange(count)
    angle = np.pi / (4 * count) * ((2 * rank[:, None] + 1) * (2 * rank[None, :] + 1) % (8 * count))
    return np.cos(angle) * (2.0 / count) ** 0.5


def halves(table):
    table = table.astype(np.float32)
    high = table.astype(ml_dtypes.bfloat16)
    low = (table - high.astype(np.float32)).astype(ml_dtypes.bfloat16)
    return np.stack([high, low])


def tables():
    full = cosines(256)
    h, r, i = np.meshgrid(np.arange(2), np.arange(16), np.arange(8), indexing="ij")
    rows = (r * 16 + h * 8 + i).reshape(-1)
    s, z, j = np.meshgrid(np.arange(2), np.arange(8), np.arange(16), indexing="ij")
    lanes = ((z * 2 + s) * 16 + j).reshape(-1)
    big = np.stack([halves(full[lanes, :]), halves(full[:, rows]), halves(full[rows, :]), halves(full[:, lanes])])
    return halves(cosines(128)), big


def split(value):
    high = value.astype(BF16)
    return high, (value - high.astype(F32)).astype(BF16)


def dot3(left, right, dims=(((1,), (0,)), ((), ()))):
    def dot(a, b):
        return lax.dot_general(a, b, dims, preferred_element_type=F32)

    return dot(left[0], right[0]) + (dot(left[0], right[1]) + dot(left[1], right[0]))


def swap_blocks(value):
    sub = lax.broadcasted_iota(jnp.int32, value.shape, 1)
    lane = lax.broadcasted_iota(jnp.int32, value.shape, 2) // 16
    for bit in (4, 2, 1):
        s_on = (sub // bit) % 2
        l_on = (lane // bit) % 2
        down = pltpu.roll(pltpu.roll(value, bit, 1), 128 - 16 * bit, 2)
        up = down if bit == 4 else pltpu.roll(pltpu.roll(value, 8 - bit, 1), 16 * bit, 2)
        value = jnp.where(s_on == l_on, value, jnp.where(s_on == 1, down, up))
    return value


def kernel(t_hbm, sx_hbm, sy_hbm, sz_hbm, hx_hbm, big_hbm, out_ref, *scratch):
    (t, sx, sy, sz, hx, big, scale, plane, mixed) = scratch[:9]
    m, ra, sb, rb, sb2, rb2, sa2, ra2 = (scratch[9 + 2 * k : 11 + 2 * k] for k in range(8))
    in_sem, send, recv = scratch[25:]

    r = lax.axis_index("row")
    c = lax.axis_index("col")
    core = lax.rem(r, 2)
    x0 = lax.rem(r // 2, 2)
    x1 = lax.rem(r // 4, 2)
    y0 = r // 8
    y2 = lax.rem(c, 2)
    z0 = lax.rem(c // 2, 2)
    z1 = lax.rem(c // 4, 2)
    z2 = c // 8
    alpha = lax.rem(y0 + y2, 2)
    my_a = core * 8 + x1 * 4 + x0 * 2 + alpha
    my_b = z2 * 8 + z1 * 4 + z0 * 2 + y0
    a_bits = {
        8: (1 - 2 * core, None, 8 - 16 * core),
        4: (4 - 8 * x1, None, 4 - 8 * x1),
        2: (2 - 4 * x0, None, 2 - 4 * x0),
        1: (None, 1 - 2 * y2, 1 - 2 * alpha),
    }
    b_bits = {
        8: (None, 8 - 16 * z2, 8 - 16 * z2),
        4: (None, 4 - 8 * z1, 4 - 8 * z1),
        2: (None, 2 - 4 * z0, 2 - 4 * z0),
        1: (8 - 16 * y0, 1 - 2 * y2, 1 - 2 * y0),
    }

    def peers(bits, own):
        found = {0: (r, c, own)}
        for mask in range(1, 16):
            bit = mask & -mask
            here = found[mask ^ bit]
            found[mask] = tuple(h if d is None else h + d for h, d in zip(here, bits[bit]))
        return [found[k] for k in (15, 14, 13, 12, 11, 10, 9, 8, 7, 6, 5, 4, 3, 2, 1)]

    a_peers = peers(a_bits, my_a)
    b_peers = peers(b_bits, my_b)

    barrier = pltpu.get_barrier_semaphore()
    for row, col, _ in b_peers + a_peers:
        pl.semaphore_signal(barrier, inc=1, device_id={"row": row, "col": col}, device_id_type=MESH)

    loads = [
        pltpu.make_async_copy(src, dst, in_sem.at[k])
        for k, (src, dst) in enumerate(
            [(t_hbm, t), (hx_hbm, hx), (sx_hbm, sx), (sy_hbm, sy), (sz_hbm, sz), (big_hbm, big)]
        )
    ]
    for load in loads:
        load.start()

    def copy(src, dst, stage, h, peer, own):
        row, col, place = peer
        return pltpu.make_async_remote_copy(
            src_ref=src[h].at[pl.ds(pl.multiple_of(place * 16, 16), 16)],
            dst_ref=dst[h].at[pl.ds(pl.multiple_of(own * 16, 16), 16)],
            send_sem=send.at[stage, h],
            recv_sem=recv.at[stage, h],
            device_id={"row": row, "col": col},
            device_id_type=MESH,
        )

    def start(src, dst, stage, h, group, own):
        for peer in group:
            copy(src, dst, stage, h, peer, own).start()
        mine = pl.ds(pl.multiple_of(own * 16, 16), 16)
        dst[h][mine, :] = src[h][mine, :]

    def whole(src, dst, stage, h):
        return pltpu.make_async_remote_copy(
            src_ref=src[h].at[pl.ds(0, 240)],
            dst_ref=dst[h].at[pl.ds(0, 240)],
            send_sem=send.at[stage, h],
            recv_sem=recv.at[stage, h],
            device_id={"row": r, "col": c},
            device_id_type=MESH,
        )

    def regroup(src, dst):
        for k in range(16):
            dst[16 * k : 16 * k + 16, :] = src[pl.ds(k, 16, stride=16), :]

    loads[0].wait()
    loads[1].wait()
    table_x = (hx[0], hx[1])
    for h in range(2):
        for f in range(2):
            lines = split(t[256 * f + 128 * h : 256 * f + 128 * h + 128, :])
            m[h][128 * f : 128 * f + 128, :] = dot3(table_x, lines, (((1,), (1,)), ((), ())))

    pl.semaphore_wait(barrier, 30)
    for h in range(2):
        start(m, ra, 0, h, a_peers, my_a)

    for load in loads[2:]:
        load.wait()
    mode = (x1 * 4 + x0 * 2 + alpha) * 16 + my_b
    at = lax.broadcasted_iota(jnp.int32, (1, 128), 1)
    part_x = jnp.sum(jnp.where(at == mode, sx[...], 0.0), axis=1, keepdims=True)
    for k in range(2):
        part_y = jnp.broadcast_to(sy[:, 128 * k : 128 * k + 128], (128, 128)).T
        for n in range(2):
            where = (slice(128 * k, 128 * k + 128), slice(128 * n, 128 * n + 128))
            scale[where] = lax.rsqrt(part_x + part_y + sz[:, 128 * n : 128 * n + 128])

    for h in range(2):
        whole(m, ra, 0, h).wait_recv()
        regroup(ra[h], sb[h])
        start(sb, rb, 1, h, b_peers, my_b)

    def at_of(k):
        row, s = k // 2, k % 2
        beta, x, own_core = row // 8, row // 2 % 4, row % 2
        return pl.ds(beta * 16 + own_core * 8 + x * 2 + (s ^ beta), 8, stride=32)

    part = [None, None]
    for h in range(2):
        whole(sb, rb, 1, h).wait_recv()
        tiles = swap_blocks(jnp.stack([rb[h][at_of(k), :] for k in range(32)]))
        for k in range(32):
            plane[8 * (k // 2) : 8 * (k // 2) + 8, 128 * (k % 2) : 128 * (k % 2) + 128] = tiles[k]
        lines = split(dot3(split(plane[...]), (big[0, 0], big[0, 1])))
        cols = slice(128 * h, 128 * h + 128)
        part[h] = dot3((big[1, 0, :, cols], big[1, 1, :, cols]), lines)
    mixed[...] = (part[0] + part[1]) * scale[...]
    modes = split(mixed[...])

    for h in range(2):
        rows = slice(128 * h, 128 * h + 128)
        lines = split(dot3((big[2, 0, rows, :], big[2, 1, rows, :]), modes))
        back = dot3(lines, (big[3, 0], big[3, 1]))
        tiles = swap_blocks(
            jnp.stack(
                [back[8 * (k // 2) : 8 * (k // 2) + 8, 128 * (k % 2) : 128 * (k % 2) + 128] for k in range(32)]
            )
        )
        for k in range(32):
            sb2[h][at_of(k), :] = tiles[k]
        start(sb2, rb2, 2, h, b_peers, my_b)

    for h in range(2):
        whole(sb2, rb2, 2, h).wait_recv()
        regroup(rb2[h], sa2[h])
        start(sa2, ra2, 3, h, a_peers, my_a)

    for h in range(2):
        whole(sa2, ra2, 3, h).wait_recv()
        for f in range(2):
            lines = split(ra2[h][128 * f : 128 * f + 128, :].T)
            out_ref[256 * f + 128 * h : 256 * f + 128 * h + 128, :] = dot3(lines, table_x)

    for stage, (src, dst) in enumerate(((m, ra), (sb, rb), (sb2, rb2), (sa2, ra2))):
        for h in range(2):
            whole(src, dst, stage, h).wait_send()


def shards(tracer, symbol_x, symbol_y, symbol_z):
    table_x, big = tables()
    lines = jnp.transpose(tracer, (0, 2, 3, 1)).reshape(512, 128)
    anywhere = pl.BlockSpec(memory_space=pl.ANY)
    result = pl.pallas_call(
        kernel,
        out_shape=jax.ShapeDtypeStruct((512, 128), F32),
        in_specs=[anywhere] * 6,
        out_specs=pl.BlockSpec(memory_space=pltpu.VMEM),
        scratch_shapes=[
            pltpu.VMEM((512, 128), F32),
            pltpu.VMEM((1, 128), F32),
            pltpu.VMEM((1, 256), F32),
            pltpu.VMEM((1, 256), F32),
            pltpu.VMEM((2, 128, 128), BF16),
            pltpu.VMEM((4, 2, 256, 256), BF16),
            pltpu.VMEM((256, 256), F32),
            pltpu.VMEM((128, 256), F32),
            pltpu.VMEM((256, 256), F32),
        ]
        + [pltpu.VMEM((256, 128), F32)] * 16
        + [
            pltpu.SemaphoreType.DMA((6,)),
            pltpu.SemaphoreType.DMA((4, 2)),
            pltpu.SemaphoreType.DMA((4, 2)),
        ],
        compiler_params=pltpu.CompilerParams(collective_id=0, has_side_effects=True),
    )(
        lines,
        symbol_x.reshape(1, 128),
        symbol_y.reshape(1, 256),
        symbol_z.reshape(1, 256),
        jnp.asarray(table_x),
        jnp.asarray(big),
    )
    return jnp.transpose(result.reshape(2, 16, 16, 128), (0, 3, 1, 2))


def solution(mesh):
    in_specs = (P("unit", None, "row", "col"), P(), P(), P())
    out_specs = P("unit", None, "row", "col")
    return jax.shard_map(shards, mesh=mesh, in_specs=in_specs, out_specs=out_specs, check_vma=False)
```

time: 126 us -> 48.2 us (0.38)
  the two profiles are of different devices: /device:TPU:8 before, /device:TPU:1 now
where the time goes in v1:
time: 48.2 us; the launch traced here: 48 us
  Pallas kernels  46.4 us (96%)
  local copies, waits for them, and re-layouts  1.67 us (3%)
    pallas_call x1, Pallas kernels, shards(): pl.pallas_call(kernel, out_shape=jax.ShapeDtypeStruct((512, 128), F32), i...  46.4 us
    unnamed x1, local copies, waits for them, and re-layouts  1.67 us

profile of v1, /device:TPU:1, one launch (start us, length us, event | category | flops | bytes accessed | tf_op | source)
XLA Modules:
  0.0 48.0 jit_solution(7004612889895859603)
XLA Ops:
  0.0 46.4 %shard_map.64 = f32[512,128]{1,0:T(8,128)} custom-call(f32[512,128]{1,0:T(8,128)} %bitcast.10, f32[1,128]{1,0:T(1,128)} %bitcast.13, f32[1,256]{1,0:T(1,128)} %bitcast.11, f32[1,256]{1,0:T(1,128)} %bitcast.12, bf16[2,128,128]{2,1,0:T(8,128)(2,1)} %constant.4.clone.hx_hbm, bf16[4,2,256,256]{3,2,1,0:T(8,128)(2,1)} %constant.5.clone.big_hbm), custom_call_target="tpu_custom_call" | custom-call | tf_op jit(solution)/shard_map/pallas_call | solution.py:228
  46.4 1.7 %copy.8 = f32[2,128,16,16]{1,3,2,0:T(8,128)} copy(f32[2,128,16,16]{1,3,2,0:T(8,128)} %bitcast.9) | data formatting | bytes 524288

commit v2 on v1

--- a/solution.py
+++ b/solution.py
@@ -34,7 +34,8 @@
     s, z, j = np.meshgrid(np.arange(2), np.arange(8), np.arange(16), indexing="ij")
     lanes = ((z * 2 + s) * 16 + j).reshape(-1)
     big = np.stack([halves(full[lanes, :]), halves(full[:, rows]), halves(full[rows, :]), halves(full[:, lanes])])
-    return halves(cosines(128)), big
+    modes = cosines(128)
+    return np.stack([halves(modes), halves(modes.reshape(8, 16, 128).transpose(1, 0, 2).reshape(128, 128))]), big
 
 
 def split(value):
@@ -63,8 +64,17 @@
 
 def kernel(t_hbm, sx_hbm, sy_hbm, sz_hbm, hx_hbm, big_hbm, out_ref, *scratch):
     (t, sx, sy, sz, hx, big, scale, plane, mixed) = scratch[:9]
-    m, ra, sb, rb, sb2, rb2, sa2, ra2 = (scratch[9 + 2 * k : 11 + 2 * k] for k in range(8))
+    m, first, turned, arrived, leaving, third, turned2, home = (scratch[9 + 2 * k : 11 + 2 * k] for k in range(8))
     in_sem, send, recv = scratch[25:]
+
+    loads = [
+        pltpu.make_async_copy(src, dst, in_sem.at[k])
+        for k, (src, dst) in enumerate(
+            [(t_hbm, t), (hx_hbm, hx), (sx_hbm, sx), (sy_hbm, sy), (sz_hbm, sz), (big_hbm, big)]
+        )
+    ]
+    for load in loads:
+        load.start()
 
     r = lax.axis_index("row")
     c = lax.axis_index("col")
@@ -77,19 +87,19 @@
     z1 = lax.rem(c // 4, 2)
     z2 = c // 8
     alpha = lax.rem(y0 + y2, 2)
-    my_a = core * 8 + x1 * 4 + x0 * 2 + alpha
-    my_b = z2 * 8 + z1 * 4 + z0 * 2 + y0
+    my_a = core * 8 + x1 * 4 + x0 * 2 + y0
+    my_b = z2 * 8 + z1 * 4 + z0 * 2 + alpha
     a_bits = {
         8: (1 - 2 * core, None, 8 - 16 * core),
         4: (4 - 8 * x1, None, 4 - 8 * x1),
         2: (2 - 4 * x0, None, 2 - 4 * x0),
-        1: (None, 1 - 2 * y2, 1 - 2 * alpha),
+        1: (8 - 16 * y0, 1 - 2 * y2, 1 - 2 * y0),
     }
     b_bits = {
         8: (None, 8 - 16 * z2, 8 - 16 * z2),
         4: (None, 4 - 8 * z1, 4 - 8 * z1),
         2: (None, 2 - 4 * z0, 2 - 4 * z0),
-        1: (8 - 16 * y0, 1 - 2 * y2, 1 - 2 * y0),
+        1: (None, 1 - 2 * y2, 1 - 2 * alpha),
     }
 
     def peers(bits, own):
@@ -106,15 +116,6 @@
     barrier = pltpu.get_barrier_semaphore()
     for row, col, _ in b_peers + a_peers:
         pl.semaphore_signal(barrier, inc=1, device_id={"row": row, "col": col}, device_id_type=MESH)
-
-    loads = [
-        pltpu.make_async_copy(src, dst, in_sem.at[k])
-        for k, (src, dst) in enumerate(
-            [(t_hbm, t), (hx_hbm, hx), (sx_hbm, sx), (sy_hbm, sy), (sz_hbm, sz), (big_hbm, big)]
-        )
-    ]
-    for load in loads:
-        load.start()
 
     def copy(src, dst, stage, h, peer, own):
         row, col, place = peer
@@ -147,21 +148,27 @@
         for k in range(16):
             dst[16 * k : 16 * k + 16, :] = src[pl.ds(k, 16, stride=16), :]
 
+    groups = {"a": (a_peers, my_a), "b": (b_peers, my_b)}
+
     loads[0].wait()
     loads[1].wait()
-    table_x = (hx[0], hx[1])
+    tables_x = [(hx[h, 0], hx[h, 1]) for h in range(2)]
     for h in range(2):
         for f in range(2):
             lines = split(t[256 * f + 128 * h : 256 * f + 128 * h + 128, :])
-            m[h][128 * f : 128 * f + 128, :] = dot3(table_x, lines, (((1,), (1,)), ((), ())))
-
-    pl.semaphore_wait(barrier, 30)
-    for h in range(2):
-        start(m, ra, 0, h, a_peers, my_a)
+            found = dot3(tables_x[h], lines, (((1,), (1,)), ((), ())))
+            if h == 0:
+                m[0][128 * f : 128 * f + 128, :] = found
+            else:
+                for k in range(16):
+                    m[1][16 * k + 8 * f : 16 * k + 8 * f + 8, :] = found[8 * k : 8 * k + 8]
+        if h == 0:
+            pl.semaphore_wait(barrier, 30)
+        start(m, first, 0, h, *groups["ab"[h]])
 
     for load in loads[2:]:
         load.wait()
-    mode = (x1 * 4 + x0 * 2 + alpha) * 16 + my_b
+    mode = (x1 * 4 + x0 * 2 + y0) * 16 + my_b
     at = lax.broadcasted_iota(jnp.int32, (1, 128), 1)
     part_x = jnp.sum(jnp.where(at == mode, sx[...], 0.0), axis=1, keepdims=True)
     for k in range(2):
@@ -171,19 +178,20 @@
             scale[where] = lax.rsqrt(part_x + part_y + sz[:, 128 * n : 128 * n + 128])
 
     for h in range(2):
-        whole(m, ra, 0, h).wait_recv()
-        regroup(ra[h], sb[h])
-        start(sb, rb, 1, h, b_peers, my_b)
-
-    def at_of(k):
+        whole(m, first, 0, h).wait_recv()
+        regroup(first[h], turned[h])
+        start(turned, arrived, 1, h, *groups["ba"[h]])
+
+    def at_of(h, k):
         row, s = k // 2, k % 2
         beta, x, own_core = row // 8, row // 2 % 4, row % 2
-        return pl.ds(beta * 16 + own_core * 8 + x * 2 + (s ^ beta), 8, stride=32)
+        a, b = own_core * 8 + x * 2 + beta, s ^ beta
+        return pl.ds(b * 16 + a, 8, stride=32) if h == 0 else pl.ds(a * 16 + b, 8, stride=2)
 
     part = [None, None]
     for h in range(2):
-        whole(sb, rb, 1, h).wait_recv()
-        tiles = swap_blocks(jnp.stack([rb[h][at_of(k), :] for k in range(32)]))
+        whole(turned, arrived, 1, h).wait_recv()
+        tiles = swap_blocks(jnp.stack([arrived[h][at_of(h, k), :] for k in range(32)]))
         for k in range(32):
             plane[8 * (k // 2) : 8 * (k // 2) + 8, 128 * (k % 2) : 128 * (k % 2) + 128] = tiles[k]
         lines = split(dot3(split(plane[...]), (big[0, 0], big[0, 1])))
@@ -202,21 +210,24 @@
             )
         )
         for k in range(32):
-            sb2[h][at_of(k), :] = tiles[k]
-        start(sb2, rb2, 2, h, b_peers, my_b)
-
-    for h in range(2):
-        whole(sb2, rb2, 2, h).wait_recv()
-        regroup(rb2[h], sa2[h])
-        start(sa2, ra2, 3, h, a_peers, my_a)
-
-    for h in range(2):
-        whole(sa2, ra2, 3, h).wait_recv()
+            leaving[h][at_of(h, k), :] = tiles[k]
+        start(leaving, third, 2, h, *groups["ba"[h]])
+
+    for h in range(2):
+        whole(leaving, third, 2, h).wait_recv()
+        regroup(third[h], turned2[h])
+        start(turned2, home, 3, h, *groups["ab"[h]])
+
+    for h in range(2):
+        whole(turned2, home, 3, h).wait_recv()
         for f in range(2):
-            lines = split(ra2[h][128 * f : 128 * f + 128, :].T)
-            out_ref[256 * f + 128 * h : 256 * f + 128 * h + 128, :] = dot3(lines, table_x)
-
-    for stage, (src, dst) in enumerate(((m, ra), (sb, rb), (sb2, rb2), (sa2, ra2))):
+            if h == 0:
+                lines = home[0][128 * f : 128 * f + 128, :]
+            else:
+                lines = jnp.concatenate([home[1][16 * k + 8 * f : 16 * k + 8 * f + 8, :] for k in range(16)])
+            out_ref[256 * f + 128 * h : 256 * f + 128 * h + 128, :] = dot3(split(lines.T), tables_x[h])
+
+    for stage, (src, dst) in enumerate(((m, first), (turned, arrived), (leaving, third), (turned2, home))):
         for h in range(2):
             whole(src, dst, stage, h).wait_send()
 
@@ -235,7 +246,7 @@
             pltpu.VMEM((1, 128), F32),
             pltpu.VMEM((1, 256), F32),
             pltpu.VMEM((1, 256), F32),
-            pltpu.VMEM((2, 128, 128), BF16),
+            pltpu.VMEM((2, 2, 128, 128), BF16),
             pltpu.VMEM((4, 2, 256, 256), BF16),
             pltpu.VMEM((256, 256), F32),
             pltpu.VMEM((128, 256), F32),

time: 48.2 us -> 45.9 us (0.952)
  Pallas kernels: 46.4 us -> 44.1 us
    pallas_call x1, Pallas kernels: 46.4 us -> 44.1 us  [shards(): pl.pallas_call(kernel, out_shape=jax.ShapeDtypeStruct((512, 128), F32), i...]
where the time goes in v2:
time: 45.9 us; the launch traced here: 45.8 us
  Pallas kernels  44.1 us (96%)
  local copies, waits for them, and re-layouts  1.67 us (4%)
    pallas_call x1, Pallas kernels, shards(): pl.pallas_call(kernel, out_shape=jax.ShapeDtypeStruct((512, 128), F32), i...  44.1 us
    unnamed x1, local copies, waits for them, and re-layouts  1.67 us

profile of v2, /device:TPU:1, one launch (start us, length us, event | category | flops | bytes accessed | tf_op | source)
XLA Modules:
  0.0 45.8 jit_solution(4494968035259194678)
XLA Ops:
  0.0 44.1 %shard_map.64 = f32[512,128]{1,0:T(8,128)} custom-call(f32[512,128]{1,0:T(8,128)} %bitcast.10, f32[1,128]{1,0:T(1,128)} %bitcast.13, f32[1,256]{1,0:T(1,128)} %bitcast.11, f32[1,256]{1,0:T(1,128)} %bitcast.12, bf16[2,2,128,128]{3,2,1,0:T(8,128)(2,1)} %constant.4.clone.hx_hbm, bf16[4,2,256,256]{3,2,1,0:T(8,128)(2,1)} %constant.5.clone.big_hbm), custom_call_target="tpu_custom_call" | custom-call | tf_op jit(solution)/shard_map/pallas_call | solution.py:239
  44.1 1.7 %copy.8 = f32[2,128,16,16]{1,3,2,0:T(8,128)} copy(f32[2,128,16,16]{1,3,2,0:T(8,128)} %bitcast.9) | data formatting | bytes 524288

commit v3 on v2

--- a/solution.py
+++ b/solution.py
@@ -238,7 +238,7 @@
     anywhere = pl.BlockSpec(memory_space=pl.ANY)
     result = pl.pallas_call(
         kernel,
-        out_shape=jax.ShapeDtypeStruct((512, 128), F32),
+        out_shape=pltpu.VMEM((512, 128), F32),
         in_specs=[anywhere] * 6,
         out_specs=pl.BlockSpec(memory_space=pltpu.VMEM),
         scratch_shapes=[

time: 45.9 us -> 44.2 us (0.963)
  local copies, waits for them, and re-layouts: 1.67 us -> 0.71 us
  Pallas kernels: 44.1 us -> 43.4 us
    unnamed x1, local copies, waits for them, and re-layouts: 1.67 us -> 0.71 us
    pallas_call x1, Pallas kernels: 44.1 us -> 43.4 us  [shards(): pl.pallas_call(kernel, out_shape=pltpu.VMEM((512, 128), F32), in_specs=[a...]
where the time goes in v3:
time: 44.2 us; the launch traced here: 44.1 us
  Pallas kernels  43.4 us (98%)
  local copies, waits for them, and re-layouts  0.71 us (2%)
    pallas_call x1, Pallas kernels, shards(): pl.pallas_call(kernel, out_shape=pltpu.VMEM((512, 128), F32), in_specs=[a...  43.4 us

profile of v3, /device:TPU:1, one launch (start us, length us, event | category | flops | bytes accessed | tf_op | source)
XLA Modules:
  0.0 44.1 jit_solution(6321349811998265954)
XLA Ops:
  0.0 43.4 %shard_map.64 = f32[512,128]{1,0:T(8,128)S(1)} custom-call(f32[512,128]{1,0:T(8,128)} %bitcast.10, f32[1,128]{1,0:T(1,128)} %bitcast.13, f32[1,256]{1,0:T(1,128)} %bitcast.11, f32[1,256]{1,0:T(1,128)} %bitcast.12, bf16[2,2,128,128]{3,2,1,0:T(8,128)(2,1)} %constant.4.clone.hx_hbm, bf16[4,2,256,256]{3,2,1,0:T(8,128)(2,1)} %constant.5.clone.big_hbm), custom_call_target="tpu_custom_call" | custom-call | tf_op jit(solution)/shard_map/pallas_call | solution.py:239
  43.4 0.7 %copy.8 = f32[2,128,16,16]{1,3,2,0:T(8,128)} copy(f32[2,128,16,16]{1,3,2,0:T(8,128)S(1)} %bitcast.9) | data formatting | bytes 524288

commit v4 on v3

--- a/solution.py
+++ b/solution.py
@@ -44,10 +44,10 @@
 
 
 def dot3(left, right, dims=(((1,), (0,)), ((), ()))):
-    def dot(a, b):
-        return lax.dot_general(a, b, dims, preferred_element_type=F32)
-
-    return dot(left[0], right[0]) + (dot(left[0], right[1]) + dot(left[1], right[0]))
+    (l_dim,), (r_dim,) = dims[0]
+    left = jnp.concatenate([left[0], left[0], left[1]], axis=l_dim)
+    right = jnp.concatenate([right[0], right[1], right[0]], axis=r_dim)
+    return lax.dot_general(left, right, dims, preferred_element_type=F32)
 
 
 def swap_blocks(value):
@@ -102,16 +102,16 @@
         1: (None, 1 - 2 * y2, 1 - 2 * alpha),
     }
 
-    def peers(bits, own):
+    def peers(bits, own, order):
         found = {0: (r, c, own)}
         for mask in range(1, 16):
             bit = mask & -mask
             here = found[mask ^ bit]
             found[mask] = tuple(h if d is None else h + d for h, d in zip(here, bits[bit]))
-        return [found[k] for k in (15, 14, 13, 12, 11, 10, 9, 8, 7, 6, 5, 4, 3, 2, 1)]
-
-    a_peers = peers(a_bits, my_a)
-    b_peers = peers(b_bits, my_b)
+        return [found[k] for k in order]
+
+    a_peers = peers(a_bits, my_a, range(15, 0, -1))
+    b_peers = peers(b_bits, my_b, (9, 10, 8, 11, 7, 12, 6, 13, 5, 14, 4, 15, 3, 2, 1))
 
     barrier = pltpu.get_barrier_semaphore()
     for row, col, _ in b_peers + a_peers:

time: 44.2 us -> 43.8 us (level)
  no operation moved by 1% of the time
where the time goes in v4:
time: 43.8 us; the launch traced here: 43.7 us
  Pallas kernels  43 us (98%)
  local copies, waits for them, and re-layouts  0.71 us (2%)
    pallas_call x1, Pallas kernels, shards(): pl.pallas_call(kernel, out_shape=pltpu.VMEM((512, 128), F32), in_specs=[a...  43 us

profile of v4, /device:TPU:1, one launch (start us, length us, event | category | flops | bytes accessed | tf_op | source)
XLA Modules:
  0.0 43.7 jit_solution(15703741644443360311)
XLA Ops:
  0.0 43.0 %shard_map.64 = f32[512,128]{1,0:T(8,128)S(1)} custom-call(f32[512,128]{1,0:T(8,128)} %bitcast.10, f32[1,128]{1,0:T(1,128)} %bitcast.13, f32[1,256]{1,0:T(1,128)} %bitcast.11, f32[1,256]{1,0:T(1,128)} %bitcast.12, bf16[2,2,128,128]{3,2,1,0:T(8,128)(2,1)} %constant.4.clone.hx_hbm, bf16[4,2,256,256]{3,2,1,0:T(8,128)(2,1)} %constant.5.clone.big_hbm), custom_call_target="tpu_custom_call" | custom-call | tf_op jit(solution)/shard_map/pallas_call | solution.py:239
  43.0 0.7 %copy.8 = f32[2,128,16,16]{1,3,2,0:T(8,128)} copy(f32[2,128,16,16]{1,3,2,0:T(8,128)S(1)} %bitcast.9) | data formatting | bytes 524288

commit v5 on v4

--- a/solution.py
+++ b/solution.py
@@ -63,9 +63,9 @@
 
 
 def kernel(t_hbm, sx_hbm, sy_hbm, sz_hbm, hx_hbm, big_hbm, out_ref, *scratch):
-    (t, sx, sy, sz, hx, big, scale, plane, mixed) = scratch[:9]
-    m, first, turned, arrived, leaving, third, turned2, home = (scratch[9 + 2 * k : 11 + 2 * k] for k in range(8))
-    in_sem, send, recv = scratch[25:]
+    (t, sx, sy, sz, hx, big, scale, plane) = scratch[:8]
+    m, first, turned, arrived, leaving, third, turned2, home = (scratch[8 + 2 * k : 10 + 2 * k] for k in range(8))
+    in_sem, send, recv = scratch[24:]
 
     loads = [
         pltpu.make_async_copy(src, dst, in_sem.at[k])
@@ -197,8 +197,7 @@
         lines = split(dot3(split(plane[...]), (big[0, 0], big[0, 1])))
         cols = slice(128 * h, 128 * h + 128)
         part[h] = dot3((big[1, 0, :, cols], big[1, 1, :, cols]), lines)
-    mixed[...] = (part[0] + part[1]) * scale[...]
-    modes = split(mixed[...])
+    modes = split((part[0] + part[1]) * scale[...])
 
     for h in range(2):
         rows = slice(128 * h, 128 * h + 128)
@@ -250,7 +249,6 @@
             pltpu.VMEM((4, 2, 256, 256), BF16),
             pltpu.VMEM((256, 256), F32),
             pltpu.VMEM((128, 256), F32),
-            pltpu.VMEM((256, 256), F32),
         ]
         + [pltpu.VMEM((256, 128), F32)] * 16
         + [

time: 43.8 us -> 43.8 us (level)
  no operation moved by 1% of the time
where the time goes in v5:
time: 43.8 us; the launch traced here: 43.7 us
  Pallas kernels  43 us (98%)
  local copies, waits for them, and re-layouts  0.71 us (2%)
    pallas_call x1, Pallas kernels, shards(): pl.pallas_call(kernel, out_shape=pltpu.VMEM((512, 128), F32), in_specs=[a...  43 us

profile of v5, /device:TPU:1, one launch (start us, length us, event | category | flops | bytes accessed | tf_op | source)
XLA Modules:
  0.0 43.7 jit_solution(15703741644443360311)
XLA Ops:
  0.0 43.0 %shard_map.64 = f32[512,128]{1,0:T(8,128)S(1)} custom-call(f32[512,128]{1,0:T(8,128)} %bitcast.10, f32[1,128]{1,0:T(1,128)} %bitcast.13, f32[1,256]{1,0:T(1,128)} %bitcast.11, f32[1,256]{1,0:T(1,128)} %bitcast.12, bf16[2,2,128,128]{3,2,1,0:T(8,128)(2,1)} %constant.4.clone.hx_hbm, bf16[4,2,256,256]{3,2,1,0:T(8,128)(2,1)} %constant.5.clone.big_hbm), custom_call_target="tpu_custom_call" | custom-call | tf_op jit(solution)/shard_map/pallas_call | solution.py:238
  43.0 0.7 %copy.8 = f32[2,128,16,16]{1,3,2,0:T(8,128)} copy(f32[2,128,16,16]{1,3,2,0:T(8,128)S(1)} %bitcast.9) | data formatting | bytes 524288
